TPU v7x, 32 devices: a whole 2x2x4 slice. The times are simulated.
32 devices in a mesh: corner: 2 (over y), gx: 16 (over z, x, core).
Axes of the slice: x: 2, y: 2, z: 4, core: 2. Of those that a mesh axis runs over, the one named last changes fastest.
Arguments:
- forward_field: float32 [6, 256, 32, 128], P(None, ('corner', 'gx')), parts along dimension 1, may hold values from -180 to 180, as said below
- adjoint_field: float32 [6, 256, 32, 128], P(None, ('corner', 'gx')), parts along dimension 1, may hold values from -6 to 6
- level_set: float32 [128, 32, 128], P('gx'), may hold values from -8 to 8
- region_labels: int32 [128, 32, 128], P('gx'), may hold values from 0 to 3
- upwind_signs: int32 [3, 128, 32, 128], P(None, 'gx'), may hold values from -1 to 1, as said below
- contrast: float32 [8], P('corner'), parts along dimension 0, may hold values from -3 to 3
- line_decay: float32 [32, 128], replicated, may hold values from 0.00078125 to 0.0625
Outputs:
- moved: float32 [256, 32, 128], P(('corner', 'gx')), parts along dimension 0
- speed: float32 [256, 32, 128], P(('corner', 'gx')), parts along dimension 0
There are 2 independent parts, one for each index of `corner`. A program takes and returns all parts, laid end to end along the dimension named above; an argument that names none is the same for every part. Nothing has to cross between parts.
Inputs may be any that keep to these rules, and one draw needn't show every extreme that they name: `forward_field`: forward field of each cell. `upwind_signs`: upwind sign of each cell along each of the three dimensions.
All inputs are finite; a program needn't handle non-finite values.
Results may differ from a plain program's by a relative error of at most 0.0003.
Values sent between devices are 32-bit elements; how exact they have to be, the bound alone decides.
A program may use at most 64 MiB of HBM per device.

v0:
```python
import math

import jax
import jax.numpy as jnp
from jax import lax
from jax.sharding import PartitionSpec as P

ITERS = 2
REGIONS = 4


weno_eps = 1e-06
redist_step = 0.3
move_step = 0.5
cross_step = 0.3
norm_floor = 0.5
half_log = math.log(1.5)
third_log = math.log(3.0)


def carried_in(part, axis, combine, identity, reverse):
    count = lax.axis_size(axis)
    place = lax.axis_index(axis)
    ahead = count - 1 - place if reverse else place
    gathered = jax.tree.map(lambda a: lax.all_gather(a, axis), part)
    state = jax.tree.map(lambda a, e: jnp.zeros_like(a) + jnp.asarray(e, a.dtype), part, identity)

    def one(turn, state):
        source = count - 1 - turn if reverse else turn
        return combine(
            state, jax.tree.map(lambda a: lax.dynamic_index_in_dim(a, source, 0, False), gathered)
        )

    return lax.fori_loop(0, ahead, one, state)


def with_halo(cells, sides, width):
    for axis, dim in sides:
        count = lax.axis_size(axis)
        ends = count - 1
        head = lax.slice_in_dim(cells, 0, width, axis=dim)
        tail = lax.slice_in_dim(cells, cells.shape[dim] - width, cells.shape[dim], axis=dim)
        cells = jnp.concatenate(
            [
                lax.ppermute(tail, axis, [(i, (i + 1) % count) for i in range(ends)]),
                cells,
                lax.ppermute(head, axis, [((i + 1) % count, i) for i in range(ends)]),
            ],
            axis=dim,
        )
    return cells


def weno_blend(first, second, third, fourth, fifth):
    cand_one = first / 3.0 - 7.0 * second / 6.0 + 11.0 * third / 6.0
    cand_two = -second / 6.0 + 5.0 * third / 6.0 + fourth / 3.0
    cand_three = third / 3.0 + 5.0 * fourth / 6.0 - fifth / 6.0
    rough_one = (
        13.0 / 12.0 * (first - 2.0 * second + third) ** 2
        + 0.25 * (first - 4.0 * second + 3.0 * third) ** 2
    )
    rough_two = 13.0 / 12.0 * (second - 2.0 * third + fourth) ** 2 + 0.25 * (second - fourth) ** 2
    rough_three = (
        13.0 / 12.0 * (third - 2.0 * fourth + fifth) ** 2
        + 0.25 * (3.0 * third - 4.0 * fourth + fifth) ** 2
    )
    weight_one = 0.1 / (weno_eps + rough_one) ** 2
    weight_two = 0.6 / (weno_eps + rough_two) ** 2
    weight_three = 0.3 / (weno_eps + rough_three) ** 2
    return (weight_one * cand_one + weight_two * cand_two + weight_three * cand_three) / (
        weight_one + weight_two + weight_three
    )


def slab_sides(extended):
    slopes = extended[1:] - extended[:-1]
    length = extended.shape[0] - 6

    def shifted(offset):
        return slopes[offset : offset + length]

    minus = weno_blend(shifted(0), shifted(1), shifted(2), shifted(3), shifted(4))
    plus = weno_blend(shifted(5), shifted(4), shifted(3), shifted(2), shifted(1))
    return (minus, plus)


def roll_sides(field, axis):
    slopes = jnp.roll(field, -1, axis) - field

    def shifted(offset):
        return jnp.roll(slopes, offset, axis)

    minus = weno_blend(shifted(3), shifted(2), shifted(1), slopes, shifted(-1))
    plus = weno_blend(shifted(-2), shifted(-1), slopes, shifted(1), shifted(2))
    return (minus, plus)


def godunov(pairs, sign):
    total = jnp.zeros_like(sign)
    for minus, plus in pairs:
        rising = jnp.maximum(jnp.maximum(minus, 0.0) ** 2, jnp.minimum(plus, 0.0) ** 2)
        falling = jnp.maximum(jnp.minimum(minus, 0.0) ** 2, jnp.maximum(plus, 0.0) ** 2)
        total = total + jnp.where(sign >= 0, rising, falling)
    return jnp.sqrt(total + 1e-12)


def gradient_size(extended, sign):
    core = extended[3:-3]
    return godunov((slab_sides(extended), roll_sides(core, 1), roll_sides(core, 2)), sign)


def unit_normal(extended, width):
    length = extended.shape[0] - 2 * width
    core = extended[width : width + length]
    grad_x = 0.5 * (
        extended[width + 1 : width + 1 + length] - extended[width - 1 : width - 1 + length]
    )
    grad_y = 0.5 * (jnp.roll(core, -1, 1) - jnp.roll(core, 1, 1))
    grad_z = 0.5 * (jnp.roll(core, -1, 2) - jnp.roll(core, 1, 2))
    size = jnp.maximum(jnp.sqrt(grad_x * grad_x + grad_y * grad_y + grad_z * grad_z), norm_floor)
    return (grad_x / size, grad_y / size, grad_z / size)


def redistance(extended, sign):
    core = extended[3:-3]
    return core - redist_step * sign * (gradient_size(extended, sign) - 1.0)


def rates(decay, normal_x, signs):
    base = decay[None] * (0.5 + normal_x * normal_x)
    ahead = base + jnp.where(signs > 0, 0.0, jnp.where(signs == 0, half_log, third_log))
    back = base + jnp.where(signs < 0, 0.0, jnp.where(signs == 0, half_log, third_log))
    return (ahead, back)


def coefficients(rate, speed):
    return (jnp.exp(-rate), jnp.sqrt(-jnp.expm1(-2.0 * rate)) * speed)


def cross_update(speed, normal_y, normal_z, sign_y, sign_z):
    along_y = jnp.where(
        sign_y > 0,
        speed - jnp.roll(speed, 1, 1),
        jnp.where(sign_y < 0, speed - jnp.roll(speed, -1, 1), 0.0),
    )
    along_z = jnp.where(
        sign_z > 0,
        speed - jnp.roll(speed, 1, 2),
        jnp.where(sign_z < 0, speed - jnp.roll(speed, -1, 2), 0.0),
    )
    return speed - cross_step * (jnp.abs(normal_y) * along_y + jnp.abs(normal_z) * along_z)


def compose(earlier, later):
    return (later[0] * earlier[0], later[0] * earlier[1] + later[1])


def chain(rate, speed, reverse):
    keep, push = coefficients(rate, speed)
    acc_keep, acc_push = lax.associative_scan(compose, (keep, push), reverse=reverse, axis=0)
    identity = (jnp.ones(keep.shape[1:], jnp.float32), jnp.zeros(keep.shape[1:], jnp.float32))
    if reverse:
        inflow = carried_in((acc_keep[0], acc_push[0]), "gx", compose, identity, True)
    else:
        inflow = carried_in((acc_keep[-1], acc_push[-1]), "gx", compose, identity, False)
    return acc_keep * inflow[1][None] + acc_push


def carry_speed(speed, normals, upwind_signs, line_decay):
    normal_x, normal_y, normal_z = normals
    ahead, back = rates(line_decay, normal_x, upwind_signs[0])
    speed = chain(ahead, speed, False)
    speed = chain(back, speed, True)
    return cross_update(speed, normal_y, normal_z, upwind_signs[1], upwind_signs[2])


def extend(field, width):
    return with_halo(field, (("gx", 0),), width)


def shards(
    forward_field, adjoint_field, level_set, region_labels, upwind_signs, contrast, line_decay
):
    devices = lax.axis_size("gx")
    coupling = jnp.sum(forward_field * adjoint_field, axis=0)
    material = jnp.zeros(level_set.shape, jnp.float32)
    for region in range(REGIONS):
        material = material + jnp.where(region_labels == region, contrast[region], 0.0)
    raw_speed = material * coupling
    total = lax.psum(jnp.sum(raw_speed * raw_speed), "gx")
    power = total / (level_set.size * devices)
    speed = raw_speed / jnp.sqrt(power + 1e-06)
    sign_start = level_set / jnp.sqrt(level_set * level_set + 1.0)
    level = level_set
    for step in range(ITERS):
        extended = extend(level, 3)
        speed = carry_speed(speed, unit_normal(extended, 3), upwind_signs, line_decay)
        level = redistance(extended, sign_start)
    extended = extend(level, 3)
    moved = level - move_step * speed * gradient_size(extended, speed)
    return (moved, speed)


def solution(mesh):
    return jax.shard_map(
        shards,
        mesh=mesh,
        in_specs=(
            P(None, ("corner", "gx"), None, None),
            P(None, ("corner", "gx"), None, None),
            P("gx", None, None),
            P("gx", None, None),
            P(None, "gx", None, None),
            P("corner"),
            P(),
        ),
        out_specs=(P(("corner", "gx"), None, None), P(("corner", "gx"), None, None)),
        check_vma=False,
    )
```

profile of v0, /device:TPU:0, one launch (start us, length us, event | category | flops | bytes accessed | tf_op | source)
XLA Modules:
  0.0 242.6 jit_solution(13305754787715645138)
XLA Ops:
  0.7 0.9 fusion.103
  1.5 1.3 collective-permute-start.1
  2.8 3.2 %collective-permute-start = (f32[3,32,128]{2,1,0:T(8,128)S(1)}, f32[3,32,128]{2,1,0:T(8,128)S(1)}, u32[]{:S(2)}, u32[]{:S(2)}) collective-permute-start(f32[3,32,128]{2,1,0:T(8,128)S(1)} %get-tuple-element.410), channel_id=1, source_target_pairs={{0,1},{1,2},{2,3},{3,4},{4,5},{5,6},{6,7},{7,8},{8,9},{9,10},{10,1... | collective-permute-start | bytes 147464 | tf_op jit(solution)/shard_map/ppermute | solution.py:45
  6.3 0.7 fusion.116
  7.1 0.7 copy-done.6
  7.8 3.2 %multiply_reduce_fusion.1 = f32[]{:T(128)} fusion(f32[8,32,128]{2,1,0:T(8,128)S(1)} %multiply_reduce_fusion, f32[]{:T(128)} %bitcast.13, s32[8,32,128]{2,1,0:T(8,128)S(1)} %copy-done.6, f32[]{:T(128)} %bitcast.12, f32[]{:T(128)} %bitcast.11, f32[]{:T(128)} %bitcast.10), kind=kLoop, calls=%fused_computation.107 | loop fusion | flops 458751 | bytes 262164 | tf_op jit(solution)/shard_map/reduce_sum | solution.py:190
  11.0 35.1 %psum.7 = f32[]{:T(128)} all-reduce(f32[]{:T(128)} %multiply_reduce_fusion.1), channel_id=1, replica_groups=mesh['corner'=2,'gx'=16] {'gx'}, use_global_device_ids=true, to_apply=%region_2.3 | all-reduce | flops 1 | bytes 8 | tf_op jit(solution)/shard_map/psum | solution.py:190
  47.6 2.1 multiply_subtract_fusion.2
  49.9 1.4 collective-permute-start.2
  51.4 1.3 collective-permute-start.3
  52.7 1.8 collective-permute-done.3
  55.1 0.6 fusion.97
  55.7 0.6 slice.1175
  56.3 0.6 fusion.95
  57.2 0.6 slice.1223
  57.9 0.6 slice.993
  58.5 0.6 fusion.75
  59.7 0.6 slice.958
  60.3 0.6 fusion.69
  61.0 2.7 %negate_exponential_fusion = (f32[8,32,128]{2,1,0:T(8,128)S(1)}, f32[8,32,128]{2,1,0:T(8,128)S(1)}) fusion(f32[8,32,128]{2,1,0:T(8,128)S(1)} %get-tuple-element.479, pred[1,8,32,128]{3,2,1,0:T(8,128)(4,1)S(1)} %get-tuple-element.310, pred[1,8,32,128]{3,2,1,0:T(8,128)(4,1)S(1)} %get-tuple-element.308, f32[]{:T(128)S(6)} %sqrt.42, ...), kind=kLoop, calls=%fused_computation.109 | loop fusion | flops 655360 | bytes 720916 | tf_op jit(solution)/shard_map/exp | solution.py:137
  64.1 18.8 %all_gather.28 = f32[16,32,128]{2,1,0:T(8,128)S(1)} all-gather(f32[1,32,128]{2,1,0:T(8,128)S(1)} %slice_add_fusion.12), channel_id=1, replica_groups=mesh['corner'=2,'gx'=16] {'gx'}, dimensions={0}, use_global_device_ids=true | all-gather | bytes 278528 | tf_op jit(solution)/shard_map/all_gather | solution.py:25
  83.0 18.8 %all_gather.27 = f32[16,32,128]{2,1,0:T(8,128)S(1)} all-gather(f32[1,32,128]{2,1,0:T(8,128)S(1)} %slice_add_fusion.14), channel_id=1, replica_groups=mesh['corner'=2,'gx'=16] {'gx'}, dimensions={0}, use_global_device_ids=true | all-gather | bytes 278528 | tf_op jit(solution)/shard_map/all_gather | solution.py:25
  102.1 0.6 copy-done.2
  102.7 0.8 copy-done.15
  103.9 0.8 copy-done.18
  104.7 0.7 copy-done.23
  105.5 0.7 slice-done.1
  106.3 19.4 %all_gather.29 = f32[16,32,128]{2,1,0:T(8,128)S(1)} all-gather(f32[1,32,128]{2,1,0:T(8,128)S(1)} %slice_add_fusion.10), channel_id=1, replica_groups=mesh['corner'=2,'gx'=16] {'gx'}, dimensions={0}, use_global_device_ids=true | all-gather | bytes 278528 | tf_op jit(solution)/shard_map/all_gather | solution.py:25
  125.7 18.2 %all_gather.26 = f32[16,32,128]{2,1,0:T(8,128)S(1)} all-gather(f32[1,32,128]{2,1,0:T(8,128)S(1)} %slice_add_fusion.15), channel_id=1, replica_groups=mesh['corner'=2,'gx'=16] {'gx'}, dimensions={0}, use_global_device_ids=true | all-gather | bytes 278528 | tf_op jit(solution)/shard_map/all_gather | solution.py:25
  144.8 0.7 copy-done.12
  146.5 19.3 %all_gather.30 = f32[16,32,128]{2,1,0:T(8,128)S(1)} all-gather(f32[1,32,128]{2,1,0:T(8,128)S(1)} %slice_add_fusion.8), channel_id=1, replica_groups=mesh['corner'=2,'gx'=16] {'gx'}, dimensions={0}, use_global_device_ids=true | all-gather | bytes 278528 | tf_op jit(solution)/shard_map/all_gather | solution.py:25
  165.9 18.4 %all_gather.25 = f32[16,32,128]{2,1,0:T(8,128)S(1)} all-gather(f32[1,32,128]{2,1,0:T(8,128)S(1)} %slice_add_fusion.16), channel_id=1, replica_groups=mesh['corner'=2,'gx'=16] {'gx'}, dimensions={0}, use_global_device_ids=true | all-gather | bytes 278528 | tf_op jit(solution)/shard_map/all_gather | solution.py:25
  184.5 0.6 copy-done.1
  185.2 0.8 copy-done.13
  186.3 0.8 copy-done.17
  187.1 0.7 copy-done.22
  188.0 0.7 slice-done
  188.8 19.7 %all_gather.31 = f32[16,32,128]{2,1,0:T(8,128)S(1)} all-gather(f32[1,32,128]{2,1,0:T(8,128)S(1)} %slice_add_fusion.6), channel_id=1, replica_groups=mesh['corner'=2,'gx'=16] {'gx'}, dimensions={0}, use_global_device_ids=true | all-gather | bytes 278528 | tf_op jit(solution)/shard_map/all_gather | solution.py:25
  208.5 18.1 %all_gather.24 = f32[16,32,128]{2,1,0:T(8,128)S(1)} all-gather(f32[1,32,128]{2,1,0:T(8,128)S(1)} %slice_add_fusion.17), channel_id=1, replica_groups=mesh['corner'=2,'gx'=16] {'gx'}, dimensions={0}, use_global_device_ids=true | all-gather | bytes 278528 | tf_op jit(solution)/shard_map/all_gather | solution.py:25
  226.6 0.7 while.55
  228.2 0.8 copy-done.8
  229.1 0.6 copy-done.33
  229.8 2.0 multiply_subtract_fusion.1
  232.6 2.2 collective-permute-start.4
  234.8 1.3 collective-permute-start.5
  236.2 2.6 %collective-permute-done.5 = f32[3,32,128]{2,1,0:T(8,128)S(1)} collective-permute-done((f32[3,32,128]{2,1,0:T(8,128)S(1)}, f32[3,32,128]{2,1,0:T(8,128)S(1)}, u32[]{:S(2)}, u32[]{:S(2)}) %collective-permute-start.5) | collective-permute-done | bytes 49184 | tf_op jit(solution)/shard_map/ppermute | solution.py:47
  238.9 0.7 copy-done.30
  239.6 3.1 %multiply_subtract_fusion = (f32[8,32,128]{2,1,0:T(8,128)}, f32[8,32,128]{2,1,0:T(8,128)}) fusion(f32[8,32,128]{2,1,0:T(8,128)S(1)} %multiply_subtract_fusion.1, f32[8,32,128]{2,1,0:T(8,128)S(1)} %get-tuple-element.382, f32[8,32,2]{2,1,0:T(8,128)S(1)} %get-tuple-element.384, f32[8,32,126]{2,1,0:T(8,128)S(1)} %get-tuple-element.386, ...), kind=kLoop, calls=%fused_computation.101 | loop fusion | flops 14974976 | bytes 4161536 | tf_op jit(solution)/shard_map/sub | solution.py:200
  (270 shorter events, 8.2 us)
Async XLA Ops:
  0.6 5.4 %copy-start = (f32[8,32,128]{2,1,0:T(8,128)S(1)}, f32[8,32,128]{2,1,0:T(8,128)}, u32[]{:S(2)}) copy-start(f32[8,32,128]{2,1,0:T(8,128)} %param.17) | copy-start | bytes 393220
  0.6 5.6 %copy-start.35 = (f32[4]{0:T(128)S(1)}, f32[4]{0:T(128)}, u32[]{:S(2)}) copy-start(f32[4]{0:T(128)} %param.20) | copy-start | bytes 52
  1.5 46.1 %collective-permute-start.1 = (f32[3,32,128]{2,1,0:T(8,128)S(1)}, f32[3,32,128]{2,1,0:T(8,128)S(1)}, u32[]{:S(2)}, u32[]{:S(2)}) collective-permute-start(f32[3,32,128]{2,1,0:T(8,128)S(1)} %get-tuple-element.409), channel_id=1, source_target_pairs={{1,0},{2,1},{3,2},{4,3},{5,4},{6,5},{7,6},{8,7},{9,8},{10,9},{11,1... | collective-permute-start | bytes 147464 | tf_op jit(solution)/shard_map/ppermute | solution.py:47
  2.8 4.1 %copy-start.3 = (f32[6,8,32,128]{3,2,1,0:T(8,128)S(1)}, f32[6,8,32,128]{3,2,1,0:T(8,128)}, u32[]{:S(2)}) copy-start(f32[6,8,32,128]{3,2,1,0:T(8,128)} %param.15) | copy-start | bytes 2359300
  2.8 4.1 %copy-start.4 = (f32[6,8,32,128]{3,2,1,0:T(8,128)S(1)}, f32[6,8,32,128]{3,2,1,0:T(8,128)}, u32[]{:S(2)}) copy-start(f32[6,8,32,128]{3,2,1,0:T(8,128)} %param.16) | copy-start | bytes 2359300
  2.8 44.0 %collective-permute-start = (f32[3,32,128]{2,1,0:T(8,128)S(1)}, f32[3,32,128]{2,1,0:T(8,128)S(1)}, u32[]{:S(2)}, u32[]{:S(2)}) collective-permute-start(f32[3,32,128]{2,1,0:T(8,128)S(1)} %get-tuple-element.410), channel_id=1, source_target_pairs={{0,1},{1,2},{2,3},{3,4},{4,5},{5,6},{6,7},{7,8},{8,9},{9,10},{10,1... | collective-permute-start | bytes 147464 | tf_op jit(solution)/shard_map/ppermute | solution.py:45
  6.9 0.9 copy-start.6
  11.0 46.0 %copy-start.19 = (f32[8,1,128]{2,1,0:T(1,128)}, f32[8,1,128]{2,1,0:T(1,128)S(1)}, u32[]{:S(2)}) copy-start(f32[8,1,128]{2,1,0:T(1,128)S(1)} %get-tuple-element.360) | copy-start | bytes 12292
  11.0 46.0 %copy-start.25 = (f32[8,1,128]{2,1,0:T(1,128)}, f32[8,1,128]{2,1,0:T(1,128)S(1)}, u32[]{:S(2)}) copy-start(f32[8,1,128]{2,1,0:T(1,128)S(1)} %get-tuple-element.359) | copy-start | bytes 12292
  46.8 10.1 %copy-start.11 = (f32[3,32,128]{2,1,0:T(8,128)}, f32[3,32,128]{2,1,0:T(8,128)S(1)}, u32[]{:S(2)}) copy-start(f32[3,32,128]{2,1,0:T(8,128)S(1)} %collective-permute-done) | copy-start | bytes 147460
  47.6 9.4 %copy-start.9 = (f32[3,32,128]{2,1,0:T(8,128)}, f32[3,32,128]{2,1,0:T(8,128)S(1)}, u32[]{:S(2)}) copy-start(f32[3,32,128]{2,1,0:T(8,128)S(1)} %collective-permute-done.1) | copy-start | bytes 147460
  49.8 4.7 %copy-start.5 = (s32[3,8,32,128]{3,2,1,0:T(8,128)S(1)}, s32[3,8,32,128]{3,2,1,0:T(8,128)}, u32[]{:S(2)}) copy-start(s32[3,8,32,128]{3,2,1,0:T(8,128)} %param.19) | copy-start | bytes 1179652
  49.9 2.8 %collective-permute-start.2 = (f32[3,32,128]{2,1,0:T(8,128)S(1)}, f32[3,32,128]{2,1,0:T(8,128)S(1)}, u32[]{:S(2)}, u32[]{:S(2)}) collective-permute-start(f32[3,32,128]{2,1,0:T(8,128)S(1)} %get-tuple-element.391), channel_id=1, source_target_pairs={{0,1},{1,2},{2,3},{3,4},{4,5},{5,6},{6,7},{7,8},{8,9},{9,10},{10,1... | collective-permute-start | bytes 147464 | tf_op jit(solution)/shard_map/ppermute | solution.py:45
  51.4 3.2 %copy-start.24 = (f32[32,128]{1,0:T(8,128)S(1)}, f32[32,128]{1,0:T(8,128)}, u32[]{:S(2)}) copy-start(f32[32,128]{1,0:T(8,128)} %param.21) | copy-start | bytes 49156
  51.4 3.1 %collective-permute-start.3 = (f32[3,32,128]{2,1,0:T(8,128)S(1)}, f32[3,32,128]{2,1,0:T(8,128)S(1)}, u32[]{:S(2)}, u32[]{:S(2)}) collective-permute-start(f32[3,32,128]{2,1,0:T(8,128)S(1)} %get-tuple-element.392), channel_id=1, source_target_pairs={{1,0},{2,1},{3,2},{4,3},{5,4},{6,5},{7,6},{8,7},{9,8},{10,9},{11,1... | collective-permute-start | bytes 147464 | tf_op jit(solution)/shard_map/ppermute | solution.py:47
  52.7 1.8 copy-start.27
  52.7 1.8 copy-start.29
  54.5 0.6 copy-start.7
  102.0 0.7 copy-start.2
  102.7 0.8 copy-start.15
  102.7 0.9 copy-start.16
  103.8 0.8 copy-start.18
  104.6 0.7 copy-start.23
  105.5 0.7 slice-start.1
  144.7 0.8 copy-start.12
  144.7 0.8 copy-start.20
  144.7 0.8 copy-start.26
  144.8 0.8 copy-start.10
  184.5 0.7 copy-start.1
  185.2 0.8 copy-start.13
  185.2 0.9 copy-start.14
  186.3 0.8 copy-start.17
  187.1 0.7 copy-start.22
  187.9 0.7 slice-start
  228.2 0.8 copy-start.8
  229.0 0.7 copy-start.33
  229.0 0.7 copy-start.34
  229.1 0.7 copy-start.21
  229.1 0.7 copy-start.32
  229.1 0.7 copy-start.31
  232.6 3.7 %collective-permute-start.4 = (f32[3,32,128]{2,1,0:T(8,128)S(1)}, f32[3,32,128]{2,1,0:T(8,128)S(1)}, u32[]{:S(2)}, u32[]{:S(2)}) collective-permute-start(f32[3,32,128]{2,1,0:T(8,128)S(1)} %get-tuple-element.371), channel_id=1, source_target_pairs={{0,1},{1,2},{2,3},{3,4},{4,5},{5,6},{6,7},{7,8},{8,9},{9,10},{10,1... | collective-permute-start | bytes 147464 | tf_op jit(solution)/shard_map/ppermute | solution.py:45
  234.8 4.0 %collective-permute-start.5 = (f32[3,32,128]{2,1,0:T(8,128)S(1)}, f32[3,32,128]{2,1,0:T(8,128)S(1)}, u32[]{:S(2)}, u32[]{:S(2)}) collective-permute-start(f32[3,32,128]{2,1,0:T(8,128)S(1)} %get-tuple-element.372), channel_id=1, source_target_pairs={{1,0},{2,1},{3,2},{4,3},{5,4},{6,5},{7,6},{8,7},{9,8},{10,9},{11,1... | collective-permute-start | bytes 147464 | tf_op jit(solution)/shard_map/ppermute | solution.py:47
  238.9 0.7 copy-start.30
  238.9 0.7 copy-start.28
where the time goes:
time: 246 us; the launch traced here: 243 us
  blocking collectives  186 us (76%)
  local copies, waits for them, and re-layouts  22 us (9%)
  other arithmetic  15.7 us (6%)
  starting transfers between devices  10.7 us (4%)
  waiting for transfers between devices  4.39 us (2%)
  between operations  2.91 us (1%)
    all_gather x8, blocking collectives, carried_in(): gathered = jax.tree.map(lambda a: lax.all_gather(a, axis), part)  151 us
    psum x1, blocking collectives, shards(): total = lax.psum(jnp.sum(raw_speed * raw_speed), 'gx')  35.1 us
    unnamed x73, local copies, waits for them, and re-layouts  10 us
    ppermute x3, starting transfers between devices, with_halo(): lax.ppermute(tail, axis, [(i, (i + 1) % count) for i in range(ends)])  6.8 us
    slice x18, local copies, waits for them, and re-layouts, chain(): lax.associative_scan(compose, (keep, push), reverse=reverse, axis=0)  5.16 us
  transfers between devices with their start and end apart: 6, of which 2 were waited for; matrix products, arithmetic and copies ran while one was open for 2% of the time, Pallas kernels for 0%

commit v1 on v0

v1 whole, which is shorter than its diff:
```python
import functools

import jax
import jax.numpy as jnp
from jax import lax
from jax.experimental import pallas as pl
from jax.experimental.pallas import tpu as pltpu
from jax.sharding import PartitionSpec as P

ITERS = 2
OWNERS = 4
MESH = pl.DeviceIdType.MESH

weno_eps = 1e-06
redist_step = 0.3
move_step = 0.5
cross_step = 0.3


def shift(a, step, axis):
    return pltpu.roll(a, (-step) % a.shape[axis], axis)


def weno_pair(d0, e0, e1, qm, q0, qp):
    c = 13.0 / 12.0
    hm, hp = 0.5 * qm, 0.5 * qp
    r1, r2, r3 = e0 + hm, 0.5 * (e0 + e1), e1 - hp
    s1 = c * qm * qm + (r1 * r1 + weno_eps)
    s2 = c * q0 * q0 + (r2 * r2 + weno_eps)
    s3 = c * qp * qp + (r3 * r3 + weno_eps)
    t1, t2, t3 = s1 * s1, s2 * s2, s3 * s3
    m1, m2, m3 = t2 * t3, t1 * t3, t1 * t2
    six = 6.0 * m2
    den_minus = m1 + six + 3.0 * m3
    den_plus = m3 + six + 3.0 * m1
    common = (2.0 * q0) * m2
    top = 1.5 * q0
    num_minus = common + m1 * (qm * (1.0 / 3.0)) + m3 * (top - hp)
    num_plus = common + m3 * (qp * (1.0 / 3.0)) + m1 * (top - hm)
    return (d0 + 0.5 * e0 + num_minus / den_minus, d0 - 0.5 * e1 + num_plus / den_plus)


def rolled_sides(f, axis):
    d0 = shift(f, 1, axis) - f
    e0 = d0 - shift(d0, -1, axis)
    e1 = shift(e0, 1, axis)
    q0 = e1 - e0
    following, plus = weno_pair(d0, e0, e1, shift(q0, -1, axis), q0, shift(q0, 1, axis))
    return shift(following, -1, axis), plus


def slab_center(ext, e, c):
    f = [ext[e, c + k] for k in range(-2, 4)]
    d = [b - a for a, b in zip(f, f[1:])]
    s = [b - a for a, b in zip(d, d[1:])]
    q = [b - a for a, b in zip(s, s[1:])]
    return weno_pair(d[2], s[1], s[2], q[0], q[1], q[2])


def loop_slab(length, ext, e, body):
    first, _ = slab_center(ext, e, 2)

    def one(i, minus_x):
        following, plus_x = slab_center(ext, e, i + 3)
        core = ext[e, i + 3]
        body(i, ((minus_x, plus_x), rolled_sides(core, 0), rolled_sides(core, 1)))
        return following

    lax.fori_loop(0, length, one, first)


def kernel(
    n, base,
    fwd_hbm, adj_hbm, lvl_hbm, lab_hbm, sgn_hbm, contrast, decay,
    moved_out, speed_out,
    fwd, adj, lab, sgn, ext, speed, kf, pf, kb, pb, kfc, cross, gain, kbc, u0, g_up, g_down,
    snd_c, snd_s, in_c, in_s, out_b, resp, pow_s, pow_in, pow_out, pow_res,
    load_sem, halo_send, halo_recv, c_send, c_recv, s_send, s_recv, r_send, r_recv,
    p_send, p_recv, q_send, q_recv,
):
    me = lax.axis_index("gx")
    corner = lax.axis_index("corner")
    length = lvl_hbm.shape[0]
    rows = lvl_hbm.shape[1] // OWNERS
    owner_no = (me - base) // 2
    is_owner = (me >= base) & (me < base + 2 * OWNERS) & (lax.rem(me - base + 2 * n, 2) == 0)

    def each(body):
        if n <= 16:
            for p in range(n):
                body(p)
        else:
            lax.fori_loop(0, n, lambda p, c: (body(p), c)[1], 0)

    loads = [
        pltpu.make_async_copy(src, dst, load_sem.at[k])
        for k, (src, dst) in enumerate((
            (lvl_hbm, ext.at[0, pl.ds(3, length)]), (fwd_hbm, fwd), (adj_hbm, adj),
            (lab_hbm, lab), (sgn_hbm, sgn)))
    ]
    for copy in loads:
        copy.start()

    barrier = pltpu.get_barrier_semaphore()

    def greet(p):
        @pl.when(p != me)
        def _():
            pl.semaphore_signal(barrier, inc=1, device_id=(corner, p), device_id_type=MESH)

    each(greet)

    @pl.when(me == 0)
    def _():
        for e in range(ITERS + 1):
            ext[e, 0:3] = jnp.zeros((3,) + ext.shape[2:], jnp.float32)

    @pl.when(me == n - 1)
    def _():
        for e in range(ITERS + 1):
            ext[e, length + 3 : length + 6] = jnp.zeros((3,) + ext.shape[2:], jnp.float32)

    loads[0].wait()
    pl.semaphore_wait(barrier, n - 1)

    def halo_copy(e, side, part):
        planes = 1 if part == 0 else 2
        if side == 0:
            src, dst = (length + 2, 2) if part == 0 else (length, 0)
        else:
            src, dst = (3, length + 3) if part == 0 else (4, length + 4)
        return pltpu.make_async_remote_copy(
            src_ref=ext.at[e, pl.ds(src, planes)],
            dst_ref=ext.at[e, pl.ds(dst, planes)],
            send_sem=halo_send.at[e, side, part],
            recv_sem=halo_recv.at[e, side, part],
            device_id=(corner, me + 1 if side == 0 else me - 1),
            device_id_type=MESH,
        )

    def halo_start(e):
        for part in range(2):
            for side in range(2):
                @pl.when((me < n - 1) if side == 0 else (me > 0))
                def _():
                    halo_copy(e, side, part).start()

    def halo_wait(e, part):
        for side in range(2):
            @pl.when((me > 0) if side == 0 else (me < n - 1))
            def _():
                halo_copy(e, side, part).wait_recv()

    halo_start(0)

    def to_owner(it, k, snd, dst, send, recv):
        owner = base + 2 * k
        src = snd.at[it, :, pl.ds(k * rows, rows), :]
        remote = pltpu.make_async_remote_copy(
            src_ref=src, dst_ref=dst.at[it, me], send_sem=send.at[it, k], recv_sem=recv.at[it],
            device_id=(corner, owner), device_id_type=MESH,
        )
        return owner, remote, pltpu.make_async_copy(src, dst.at[it, me], recv.at[it])

    def phase_one(it, snd, dst, send, recv):
        for k in range(OWNERS):
            owner, remote, local = to_owner(it, k, snd, dst, send, recv)

            @pl.when(me != owner)
            def _():
                remote.start()

            @pl.when(me == owner)
            def _():
                local.start()

    for copy in loads[1:4]:
        copy.wait()
    regions = contrast.shape[0]

    def raw(i, acc):
        coupling = fwd[0, i] * adj[0, i]
        for k in range(1, fwd.shape[0]):
            coupling = coupling + fwd[k, i] * adj[k, i]
        labels = lab[i]
        material = jnp.zeros(labels.shape, jnp.float32)
        for region in range(regions):
            material = jnp.where(labels == region, contrast[region], material)
        value = material * coupling
        speed[i] = value
        return acc + value * value

    squares = lax.fori_loop(0, length, raw, jnp.zeros(decay.shape, jnp.float32))
    tile = squares[0:8]
    for k in range(8, squares.shape[0], 8):
        tile = tile + squares[k : k + 8]
    pow_s[...] = tile

    def pow_copy():
        return pltpu.make_async_remote_copy(
            src_ref=pow_s, dst_ref=pow_in.at[me], send_sem=p_send.at[0], recv_sem=p_recv.at[0],
            device_id=(corner, base), device_id_type=MESH,
        )

    @pl.when(me != base)
    def _():
        pow_copy().start()

    @pl.when(me == base)
    def _():
        pltpu.make_async_copy(pow_s, pow_in.at[me], p_recv.at[0]).start()

    loads[4].wait()

    def coefficients(it):
        halo_wait(it, 0)

        def one(i, carry):
            f = ext[it, i + 3]
            gx = 0.5 * (ext[it, i + 4] - ext[it, i + 2])
            gy = 0.5 * (shift(f, 1, 0) - shift(f, -1, 0))
            gz = 0.5 * (shift(f, 1, 1) - shift(f, -1, 1))
            inv = lax.rsqrt(jnp.maximum(gx * gx + gy * gy + gz * gz, 0.25))
            nx = gx * inv
            y = decay[...] * (0.5 + nx * nx)
            t = y * (1.0 - y * 0.5 * (1.0 - y * (1.0 / 3.0) * (1.0 - y * 0.25 * (1.0 - y * 0.2))))
            keep = 1.0 - t
            z = t * (2.0 - t)
            sx = sgn[0, i]
            third = jnp.float32(1.0 / 3.0)
            two = jnp.float32(2.0 / 3.0)
            one_ = jnp.float32(1.0)
            mf = jnp.where(sx > 0, one_, jnp.where(sx == 0, two, third))
            mb = jnp.where(sx < 0, one_, jnp.where(sx == 0, two, third))
            a9, a4 = jnp.float32(1.0 / 9.0), jnp.float32(4.0 / 9.0)
            vf = jnp.where(sx > 0, one_, jnp.where(sx == 0, a4, a9))
            vb = jnp.where(sx < 0, one_, jnp.where(sx == 0, a4, a9))
            kf[i] = keep * mf
            kb[i] = keep * mb
            pf[i] = jnp.sqrt((1.0 - vf) + vf * z)
            pb[i] = jnp.sqrt((1.0 - vb) + vb * z)
            cross[it, 0, i] = cross_step * jnp.abs(gy * inv) * sgn[1, i].astype(jnp.float32)
            cross[it, 1, i] = cross_step * jnp.abs(gz * inv) * sgn[2, i].astype(jnp.float32)
            return carry

        lax.fori_loop(0, length, one, 0)
        run = kf[0]
        kfc[0] = run
        for i in range(1, length):
            run = run * kf[i]
            kfc[i] = run
        snd_c[it, 0] = run
        g, k = pb[length - 1] * kfc[length - 1], kb[length - 1]
        gain[it, length - 1] = g
        kbc[it, length - 1] = k
        for i in range(length - 2, -1, -1):
            g = kb[i] * g + pb[i] * kfc[i]
            k = k * kb[i]
            gain[it, i] = g
            kbc[it, i] = k
        snd_c[it, 1] = k
        snd_c[it, 2] = g
        phase_one(it, snd_c, in_c, c_send, c_recv)

    def sweeps(it):
        w = pf[0] * speed[0]
        speed[0] = w
        for i in range(1, length):
            w = kf[i] * w + pf[i] * speed[i]
            speed[i] = w
        snd_s[it, 0] = w
        u = pb[length - 1] * w
        u0[length - 1] = u
        for i in range(length - 2, -1, -1):
            u = kb[i] * u + pb[i] * speed[i]
            u0[i] = u
        snd_s[it, 1] = u
        phase_one(it, snd_s, in_s, s_send, s_recv)

    def redistance(e):
        halo_wait(e, 1)

        def body(i, pairs):
            start = ext[0, i + 3]
            up = start >= 0.0
            total = jnp.full(start.shape, 1e-12, jnp.float32)
            for minus, plus in pairs:
                other = -plus
                v = jnp.where(up, jnp.maximum(minus, other), -jnp.minimum(minus, other))
                v = jnp.maximum(v, 0.0)
                total = total + v * v
            sign = start * lax.rsqrt(start * start + 1.0)
            ext[e + 1, i + 3] = ext[e, i + 3] - redist_step * sign * (jnp.sqrt(total) - 1.0)

        loop_slab(length, ext, e, body)
        halo_start(e + 1)

    def both_sizes(e):
        halo_wait(e, 0)
        halo_wait(e, 1)

        def body(i, pairs):
            rise = jnp.full(g_up.shape[1:], 1e-12, jnp.float32)
            fall = rise
            for minus, plus in pairs:
                other = -plus
                hi = jnp.maximum(jnp.maximum(minus, other), 0.0)
                lo = jnp.minimum(jnp.minimum(minus, other), 0.0)
                rise = rise + hi * hi
                fall = fall + lo * lo
            g_up[i] = jnp.sqrt(rise)
            g_down[i] = jnp.sqrt(fall)

        loop_slab(length, ext, e, body)

    def reply(it, p):
        src = out_b.at[it, p]
        dst = resp.at[it, :, pl.ds(pl.multiple_of(owner_no * rows, rows), rows), :]
        remote = pltpu.make_async_remote_copy(
            src_ref=src, dst_ref=dst, send_sem=r_send.at[it, p], recv_sem=r_recv.at[it],
            device_id=(corner, p), device_id_type=MESH,
        )
        return remote, pltpu.make_async_copy(src, dst, r_recv.at[it])

    def own(it):
        @pl.when(is_owner)
        def _():
            pltpu.make_async_copy(in_c.at[it], in_c.at[it], c_recv.at[it]).wait()
            pltpu.make_async_copy(in_s.at[it], in_s.at[it], s_recv.at[it]).wait()
            zero = jnp.zeros(in_s.shape[3:], jnp.float32)

            def ahead(p, w):
                out_b[it, p, 0] = w
                return in_c[it, p, 0] * w + in_s[it, p, 0]

            def back(turn, u):
                p = n - 1 - turn
                out_b[it, p, 1] = u
                return in_c[it, p, 1] * u + (in_c[it, p, 2] * out_b[it, p, 0] + in_s[it, p, 1])

            lax.fori_loop(0, n, ahead, zero, unroll=n <= 16)
            lax.fori_loop(0, n, back, zero, unroll=n <= 16)

            def send(p):
                remote, local = reply(it, p)

                @pl.when(p != me)
                def _():
                    remote.start()

                @pl.when(p == me)
                def _():
                    local.start()

            each(send)

    def pow_reply(p):
        remote = pltpu.make_async_remote_copy(
            src_ref=pow_out, dst_ref=pow_res, send_sem=q_send.at[p], recv_sem=q_recv.at[0],
            device_id=(corner, p), device_id_type=MESH,
        )
        return remote, pltpu.make_async_copy(pow_out, pow_res, q_recv.at[0])

    def own_power():
        @pl.when(me == base)
        def _():
            pltpu.make_async_copy(pow_in, pow_in, p_recv.at[0]).wait()
            pow_out[...] = lax.fori_loop(
                0, n, lambda p, acc: acc + pow_in[p], jnp.zeros(pow_out.shape, jnp.float32)
            )

            def send(p):
                remote, local = pow_reply(p)

                @pl.when(p != me)
                def _():
                    remote.start()

                @pl.when(p == me)
                def _():
                    local.start()

            each(send)

    def finish(it, body):
        pltpu.make_async_copy(resp.at[it], resp.at[it], r_recv.at[it]).wait()

        def one(i, carry):
            s = u0[i] + gain[it, i] * resp[it, 0] + kbc[it, i] * resp[it, 1]
            cy, cz = cross[it, 0, i], cross[it, 1, i]
            near_y = jnp.where(cy > 0.0, shift(s, -1, 0), shift(s, 1, 0))
            near_z = jnp.where(cz > 0.0, shift(s, -1, 1), shift(s, 1, 1))
            body(i, s - (jnp.abs(cy) * (s - near_y) + jnp.abs(cz) * (s - near_z)))
            return carry

        lax.fori_loop(0, length, one, 0)

    def keep_speed(i, s):
        speed[i] = s

    coefficients(0)
    sweeps(0)
    for it in range(ITERS):
        last = it == ITERS - 1
        if not last:
            redistance(it)
            own(it)
            if it == 0:
                own_power()
            coefficients(it + 1)
            if it + 1 == ITERS - 1:
                redistance(it + 1)
            finish(it, keep_speed)
            sweeps(it + 1)
        else:
            both_sizes(it + 1)
            own(it)

    pltpu.make_async_copy(pow_res, pow_res, q_recv.at[0]).wait()
    cells = length * decay.shape[0] * decay.shape[1] * n
    total = jnp.sum(pow_res[...], keepdims=True)
    scale = lax.rsqrt(total * (1.0 / cells) + 1e-06)

    def emit(i, s):
        s = s * scale
        speed_out[i] = s
        size = jnp.where(s >= 0.0, g_up[i], g_down[i])
        moved_out[i] = ext[ITERS, i + 3] - move_step * s * size

    finish(ITERS - 1, emit)

    for e in range(ITERS + 1):
        for part in range(2):
            for side in range(2):
                @pl.when((me < n - 1) if side == 0 else (me > 0))
                def _():
                    halo_copy(e, side, part).wait_send()

    for it in range(ITERS):
        for k in range(OWNERS):
            for args in ((snd_c, in_c, c_send, c_recv), (snd_s, in_s, s_send, s_recv)):
                owner, remote, _ = to_owner(it, k, *args)

                @pl.when(me != owner)
                def _():
                    remote.wait_send()

    @pl.when(me != base)
    def _():
        pow_copy().wait_send()

    @pl.when(is_owner)
    def _():
        for it in range(ITERS):
            def done(p):
                @pl.when(p != me)
                def _():
                    reply(it, p)[0].wait_send()

            each(done)

    @pl.when(me == base)
    def _():
        def done(p):
            @pl.when(p != me)
            def _():
                pow_reply(p)[0].wait_send()

        each(done)


def solution(mesh):
    n = mesh.shape["gx"]
    base = n // 2 - OWNERS

    def shards(forward, adjoint, level, labels, signs, contrast, decay):
        slab = level.shape
        length, depth, height = slab
        rows = depth // OWNERS
        f32 = jnp.float32
        vm = lambda *shape: pltpu.VMEM(shape, f32)
        sems = lambda *shape: pltpu.SemaphoreType.DMA(shape)
        any_ = pl.BlockSpec(memory_space=pl.ANY)
        vmem = pl.BlockSpec(memory_space=pltpu.VMEM)
        return pl.pallas_call(
            functools.partial(kernel, n, base),
            out_shape=(jax.ShapeDtypeStruct(slab, f32), jax.ShapeDtypeStruct(slab, f32)),
            in_specs=[any_] * 5 + [pl.BlockSpec(memory_space=pltpu.SMEM), vmem],
            out_specs=(vmem, vmem),
            scratch_shapes=[
                vm(*forward.shape), vm(*adjoint.shape),
                pltpu.VMEM(slab, jnp.int32), pltpu.VMEM(signs.shape, jnp.int32),
                vm(ITERS + 1, length + 6, depth, height),
                vm(*slab), vm(*slab), vm(*slab), vm(*slab), vm(*slab), vm(*slab),
                vm(ITERS, 2, *slab), vm(ITERS, *slab), vm(ITERS, *slab), vm(*slab),
                vm(*slab), vm(*slab),
                vm(ITERS, 3, depth, height), vm(ITERS, 2, depth, height),
                vm(ITERS, n, 3, rows, height), vm(ITERS, n, 2, rows, height),
                vm(ITERS, n, 2, rows, height), vm(ITERS, 2, depth, height),
                vm(8, height), vm(n, 8, height), vm(8, height), vm(8, height),
                sems(5), sems(ITERS + 1, 2, 2), sems(ITERS + 1, 2, 2),
                sems(ITERS, OWNERS), sems(ITERS), sems(ITERS, OWNERS), sems(ITERS),
                sems(ITERS, n), sems(ITERS), sems(1), sems(1), sems(n), sems(1),
            ],
            compiler_params=pltpu.CompilerParams(collective_id=0, has_side_effects=True),
        )(forward, adjoint, level, labels, signs, contrast, decay)

    return jax.shard_map(
        shards,
        mesh=mesh,
        in_specs=(
            P(None, ("corner", "gx"), None, None),
            P(None, ("corner", "gx"), None, None),
            P("gx", None, None),
            P("gx", None, None),
            P(None, "gx", None, None),
            P("corner"),
            P(),
        ),
        out_specs=(P(("corner", "gx"), None, None), P(("corner", "gx"), None, None)),
        check_vma=False,
    )
```

time: 246 us -> 35.7 us (0.15); the launches traced: 243 us -> 35.5 us
  blocking collectives: 186 us -> 0 us
  Pallas kernels: 0 us -> 32.6 us
  local copies, waits for them, and re-layouts: 22 us -> 2.26 us
  other arithmetic: 15.7 us -> 0 us
  starting transfers between devices: 10.7 us -> 0 us
  waiting for transfers between devices: 4.39 us -> 0 us
    all_gather x8 -> x0, blocking collectives: 151 us -> none  [carried_in(): gathered = jax.tree.map(lambda a: lax.all_gather(a, axis), part)]
    psum x1 -> x0, blocking collectives: 35.1 us -> none  [shards(): total = lax.psum(jnp.sum(raw_speed * raw_speed), 'gx')]
    pallas_call x0 -> x1, Pallas kernels: none -> 32.6 us  [shards(): pl.pallas_call(functools.partial(kernel, n, base), out_shape=(jax.ShapeDt...]
    slice x71 -> x0, local copies, waits for them, and re-layouts: 11 us -> none  [the longest x18 5.16 us: chain(): lax.associative_scan(compose, (keep, push), reverse=reverse, axis=0)]
    ppermute x6 -> x0, starting transfers between devices: 10.7 us -> none  [the longest x3 6.8 us: with_halo(): lax.ppermute(tail, axis, [(i, (i + 1) % count) for i in range(ends)])]
    unnamed x73 -> x4, local copies, waits for them, and re-layouts: 10 us -> 2.26 us
    sub x7 -> x0, other arithmetic: 7.34 us -> none  [the longest x2 4.09 us: redistance(): return core - redist_step * sign * (gradient_size(extended, sign) - 1.0)]
    ppermute x6 -> x0, waiting for transfers between devices: 4.39 us -> none  [the longest x3 4.38 us: with_halo(): lax.ppermute(head, axis, [((i + 1) % count, i) for i in range(ends)])]
  transfers between devices with their start and end apart: 6 -> 0, of which waited for: 2 -> 0; matrix products, arithmetic and copies ran while one was open for 2% -> 0% of each run, Pallas kernels for 0% -> 0%
where the time goes in v1:
time: 35.7 us; the launch traced here: 35.5 us
  Pallas kernels  32.6 us (91%)
  local copies, waits for them, and re-layouts  2.26 us (6%)
  between operations  0.65 us (2%)
    pallas_call x1, Pallas kernels, shards(): pl.pallas_call(functools.partial(kernel, n, base), out_shape=(jax.ShapeDt...  32.6 us
    unnamed x4, local copies, waits for them, and re-layouts  2.26 us

profile of v1, /device:TPU:0, one launch (start us, length us, event | category | flops | bytes accessed | tf_op | source)
XLA Modules:
  0.0 35.5 jit_solution(3807517360228664540)
XLA Ops:
  0.6 32.6 %shard_map.86 = (f32[8,32,128]{2,1,0:T(8,128)}, f32[8,32,128]{2,1,0:T(8,128)}) custom-call(f32[6,8,32,128]{3,2,1,0:T(8,128)} %fwd_hbm.1, f32[6,8,32,128]{3,2,1,0:T(8,128)} %adj_hbm.1, f32[8,32,128]{2,1,0:T(8,128)} %lvl_hbm.1, s32[8,32,128]{2,1,0:T(8,128)} %lab_hbm.1, s32[3,8,32,128]{3,2,1,0:T(8,128)} %sgn_hbm.1, f32[4]{0:T(128)} %contrast.1, f32[32,128]{1,0:T(8,128)} %decay.1), custom_call_target="tpu_custom_call" | custom-call | tf_op jit(solution)/shard_map/pallas_call | solution.py:485
  33.2 0.0 copy-start
  33.2 1.6 %copy.11 = f32[8,32,128]{2,1,0:T(8,128)} copy(f32[8,32,128]{2,1,0:T(8,128)} %get-tuple-element.4) | data formatting | bytes 262144
  34.8 0.0 copy-done
  34.8 0.7 %copy.12 = f32[8,32,128]{2,1,0:T(8,128)} copy(f32[8,32,128]{2,1,0:T(8,128)S(1)} %copy-done) | data formatting | bytes 262144
Async XLA Ops:
  33.2 1.6 %copy-start = (f32[8,32,128]{2,1,0:T(8,128)S(1)}, f32[8,32,128]{2,1,0:T(8,128)}, u32[]{:S(2)}) copy-start(f32[8,32,128]{2,1,0:T(8,128)} %get-tuple-element.5) | copy-start | bytes 393220

commit v2 on v1

--- a/solution.py
+++ b/solution.py
@@ -22,22 +22,23 @@
 
 
 def weno_pair(d0, e0, e1, qm, q0, qp):
-    c = 13.0 / 12.0
-    hm, hp = 0.5 * qm, 0.5 * qp
-    r1, r2, r3 = e0 + hm, 0.5 * (e0 + e1), e1 - hp
-    s1 = c * qm * qm + (r1 * r1 + weno_eps)
-    s2 = c * q0 * q0 + (r2 * r2 + weno_eps)
-    s3 = c * qp * qp + (r3 * r3 + weno_eps)
+    c = 13.0 / 3.0
+    r1, r2, r3 = e0 + (e0 + qm), e0 + e1, e1 + (e1 - qp)
+    s1 = c * qm * qm + (r1 * r1 + 4.0 * weno_eps)
+    s2 = c * q0 * q0 + (r2 * r2 + 4.0 * weno_eps)
+    s3 = c * qp * qp + (r3 * r3 + 4.0 * weno_eps)
     t1, t2, t3 = s1 * s1, s2 * s2, s3 * s3
     m1, m2, m3 = t2 * t3, t1 * t3, t1 * t2
-    six = 6.0 * m2
-    den_minus = m1 + six + 3.0 * m3
-    den_plus = m3 + six + 3.0 * m1
-    common = (2.0 * q0) * m2
+    six, three_1, three_3 = 6.0 * m2, 3.0 * m1, 3.0 * m3
+    common = six * q0
     top = 1.5 * q0
-    num_minus = common + m1 * (qm * (1.0 / 3.0)) + m3 * (top - hp)
-    num_plus = common + m3 * (qp * (1.0 / 3.0)) + m1 * (top - hm)
-    return (d0 + 0.5 * e0 + num_minus / den_minus, d0 - 0.5 * e1 + num_plus / den_plus)
+    num_minus = m1 * qm + common + three_3 * (top - 0.5 * qp)
+    num_plus = m3 * qp + common + three_1 * (top - 0.5 * qm)
+    d3 = 3.0 * d0
+    return (
+        d3 + 1.5 * e0 + num_minus / (m1 + six + three_3),
+        d3 - 1.5 * e1 + num_plus / (m3 + six + three_1),
+    )
 
 
 def rolled_sides(f, axis):
@@ -49,34 +50,43 @@
     return shift(following, -1, axis), plus
 
 
-def slab_center(ext, e, c):
-    f = [ext[e, c + k] for k in range(-2, 4)]
-    d = [b - a for a, b in zip(f, f[1:])]
-    s = [b - a for a, b in zip(d, d[1:])]
-    q = [b - a for a, b in zip(s, s[1:])]
-    return weno_pair(d[2], s[1], s[2], q[0], q[1], q[2])
-
-
-def loop_slab(length, ext, e, body):
-    first, _ = slab_center(ext, e, 2)
-
-    def one(i, minus_x):
-        following, plus_x = slab_center(ext, e, i + 3)
-        core = ext[e, i + 3]
-        body(i, ((minus_x, plus_x), rolled_sides(core, 0), rolled_sides(core, 1)))
-        return following
-
-    lax.fori_loop(0, length, one, first)
+def slab_pass(length, ext, e, body):
+    for r in range(0, ext.shape[2], 8):
+        at = slice(r, r + 8)
+        f = [ext[e, c, at] for c in range(length + 6)]
+        d = [b - a for a, b in zip(f, f[1:])]
+        s = [b - a for a, b in zip(d, d[1:])]
+        q = [b - a for a, b in zip(s, s[1:])]
+        minus = None
+        for c in range(2, length + 3):
+            following, plus = weno_pair(d[c], s[c - 1], s[c], q[c - 2], q[c - 1], q[c])
+            if c > 2:
+                body(c - 3, at, minus, plus)
+            minus = following
+
+
+def planes(length, body, unroll):
+    if unroll == length:
+        for i in range(length):
+            body(i)
+    else:
+        def some(j, carry):
+            for k in range(unroll):
+                body(j * unroll + k)
+            return carry
+
+        lax.fori_loop(0, length // unroll, some, 0)
 
 
 def kernel(
     n, base,
-    fwd_hbm, adj_hbm, lvl_hbm, lab_hbm, sgn_hbm, contrast, decay,
-    moved_out, speed_out,
+    fwd_hbm, adj_hbm, lvl_hbm, lab_hbm, sgn_hbm, contrast_hbm, decay_hbm,
+    moved_hbm, speed_hbm,
+    contrast, decay, moved_out, speed_out, base_size,
     fwd, adj, lab, sgn, ext, speed, kf, pf, kb, pb, kfc, cross, gain, kbc, u0, g_up, g_down,
     snd_c, snd_s, in_c, in_s, out_b, resp, pow_s, pow_in, pow_out, pow_res,
     load_sem, halo_send, halo_recv, c_send, c_recv, s_send, s_recv, r_send, r_recv,
-    p_send, p_recv, q_send, q_recv,
+    p_send, p_recv, q_send, q_recv, out_sem,
 ):
     me = lax.axis_index("gx")
     corner = lax.axis_index("corner")
@@ -95,16 +105,22 @@
     loads = [
         pltpu.make_async_copy(src, dst, load_sem.at[k])
         for k, (src, dst) in enumerate((
-            (lvl_hbm, ext.at[0, pl.ds(3, length)]), (fwd_hbm, fwd), (adj_hbm, adj),
-            (lab_hbm, lab), (sgn_hbm, sgn)))
+            (lvl_hbm, ext.at[0, pl.ds(3, length)]), (sgn_hbm, sgn), (decay_hbm, decay),
+            (contrast_hbm, contrast), (lab_hbm, lab), (fwd_hbm, fwd), (adj_hbm, adj)))
     ]
     for copy in loads:
         copy.start()
 
     barrier = pltpu.get_barrier_semaphore()
 
+    def is_own(p):
+        return (p >= base) & (p < base + 2 * OWNERS) & (lax.rem(p - base + 2 * n, 2) == 0)
+
     def greet(p):
-        @pl.when(p != me)
+        p = jnp.int32(p)
+        meets = is_owner | is_own(p) | (p == me - 1) | (p == me + 1)
+
+        @pl.when((p != me) & meets)
         def _():
             pl.semaphore_signal(barrier, inc=1, device_id=(corner, p), device_id_type=MESH)
 
@@ -120,8 +136,10 @@
         for e in range(ITERS + 1):
             ext[e, length + 3 : length + 6] = jnp.zeros((3,) + ext.shape[2:], jnp.float32)
 
-    loads[0].wait()
-    pl.semaphore_wait(barrier, n - 1)
+    def beside(p, inside):
+        return (inside & jnp.logical_not(is_own(p))).astype(jnp.int32)
+
+    met = jnp.where(is_owner, n - 1, OWNERS + beside(me - 1, me > 0) + beside(me + 1, me < n - 1))
 
     def halo_copy(e, side, part):
         planes = 1 if part == 0 else 2
@@ -151,8 +169,6 @@
             def _():
                 halo_copy(e, side, part).wait_recv()
 
-    halo_start(0)
-
     def to_owner(it, k, snd, dst, send, recv):
         owner = base + 2 * k
         src = snd.at[it, :, pl.ds(k * rows, rows), :]
@@ -174,48 +190,43 @@
             def _():
                 local.start()
 
-    for copy in loads[1:4]:
-        copy.wait()
-    regions = contrast.shape[0]
-
-    def raw(i, acc):
-        coupling = fwd[0, i] * adj[0, i]
-        for k in range(1, fwd.shape[0]):
-            coupling = coupling + fwd[k, i] * adj[k, i]
-        labels = lab[i]
-        material = jnp.zeros(labels.shape, jnp.float32)
-        for region in range(regions):
-            material = jnp.where(labels == region, contrast[region], material)
-        value = material * coupling
-        speed[i] = value
-        return acc + value * value
-
-    squares = lax.fori_loop(0, length, raw, jnp.zeros(decay.shape, jnp.float32))
-    tile = squares[0:8]
-    for k in range(8, squares.shape[0], 8):
-        tile = tile + squares[k : k + 8]
-    pow_s[...] = tile
-
     def pow_copy():
         return pltpu.make_async_remote_copy(
             src_ref=pow_s, dst_ref=pow_in.at[me], send_sem=p_send.at[0], recv_sem=p_recv.at[0],
             device_id=(corner, base), device_id_type=MESH,
         )
 
-    @pl.when(me != base)
-    def _():
-        pow_copy().start()
-
-    @pl.when(me == base)
-    def _():
-        pltpu.make_async_copy(pow_s, pow_in.at[me], p_recv.at[0]).start()
-
-    loads[4].wait()
-
-    def coefficients(it):
-        halo_wait(it, 0)
-
-        def one(i, carry):
+    def send_power():
+        @pl.when(me != base)
+        def _():
+            pow_copy().start()
+
+        @pl.when(me == base)
+        def _():
+            pltpu.make_async_copy(pow_s, pow_in.at[me], p_recv.at[0]).start()
+
+    regions = contrast.shape[0]
+
+    def raw_speed():
+        acc = jnp.zeros(decay.shape, jnp.float32)
+        for i in range(length):
+            coupling = fwd[0, i] * adj[0, i]
+            for k in range(1, fwd.shape[0]):
+                coupling = coupling + fwd[k, i] * adj[k, i]
+            labels = lab[i]
+            material = jnp.zeros(labels.shape, jnp.float32)
+            for region in range(regions):
+                material = jnp.where(labels == region, contrast[region], material)
+            value = material * coupling
+            speed[i] = value
+            acc = acc + value * value
+        tile = acc[0:8]
+        for k in range(8, acc.shape[0], 8):
+            tile = tile + acc[k : k + 8]
+        pow_s[...] = tile
+
+    def plane_rates(it, which):
+        for i in which:
             f = ext[it, i + 3]
             gx = 0.5 * (ext[it, i + 4] - ext[it, i + 2])
             gy = 0.5 * (shift(f, 1, 0) - shift(f, -1, 0))
@@ -241,9 +252,10 @@
             pb[i] = jnp.sqrt((1.0 - vb) + vb * z)
             cross[it, 0, i] = cross_step * jnp.abs(gy * inv) * sgn[1, i].astype(jnp.float32)
             cross[it, 1, i] = cross_step * jnp.abs(gz * inv) * sgn[2, i].astype(jnp.float32)
-            return carry
-
-        lax.fori_loop(0, length, one, 0)
+
+    def coefficients(it):
+        halo_wait(it, 0)
+        plane_rates(it, (0, length - 1))
         run = kf[0]
         kfc[0] = run
         for i in range(1, length):
@@ -277,41 +289,56 @@
         snd_s[it, 1] = u
         phase_one(it, snd_s, in_s, s_send, s_recv)
 
-    def redistance(e):
+    def across(e):
+        both = e == ITERS
+
+        def body(i):
+            f = ext[e, i + 3]
+            pairs = (rolled_sides(f, 0), rolled_sides(f, 1))
+            if both:
+                rise = fall = None
+                for minus, plus in pairs:
+                    hi = jnp.maximum(jnp.maximum(minus, -plus), 0.0)
+                    lo = jnp.minimum(jnp.minimum(minus, -plus), 0.0)
+                    rise = hi * hi if rise is None else rise + hi * hi
+                    fall = lo * lo if fall is None else fall + lo * lo
+                g_up[i] = rise
+                g_down[i] = fall
+            else:
+                up = ext[0, i + 3] >= 0.0
+                total = None
+                for minus, plus in pairs:
+                    v = jnp.where(up, jnp.maximum(minus, -plus), jnp.maximum(-minus, plus))
+                    v = jnp.maximum(v, 0.0)
+                    total = v * v if total is None else total + v * v
+                base_size[i] = total
+
+        planes(length, body, 2)
+
+    def along(e):
+        both = e == ITERS
+        if both:
+            halo_wait(e, 0)
         halo_wait(e, 1)
-
-        def body(i, pairs):
-            start = ext[0, i + 3]
-            up = start >= 0.0
-            total = jnp.full(start.shape, 1e-12, jnp.float32)
-            for minus, plus in pairs:
-                other = -plus
-                v = jnp.where(up, jnp.maximum(minus, other), -jnp.minimum(minus, other))
+        ninth = 1.0 / 9.0
+
+        def body(i, at, minus, plus):
+            if both:
+                hi = jnp.maximum(jnp.maximum(minus, -plus), 0.0)
+                lo = jnp.minimum(jnp.minimum(minus, -plus), 0.0)
+                g_up[i, at] = jnp.sqrt((g_up[i, at] + hi * hi) * ninth + 1e-12)
+                g_down[i, at] = jnp.sqrt((g_down[i, at] + lo * lo) * ninth + 1e-12)
+            else:
+                start = ext[0, i + 3, at]
+                v = jnp.where(start >= 0.0, jnp.maximum(minus, -plus), jnp.maximum(-minus, plus))
                 v = jnp.maximum(v, 0.0)
-                total = total + v * v
-            sign = start * lax.rsqrt(start * start + 1.0)
-            ext[e + 1, i + 3] = ext[e, i + 3] - redist_step * sign * (jnp.sqrt(total) - 1.0)
-
-        loop_slab(length, ext, e, body)
-        halo_start(e + 1)
-
-    def both_sizes(e):
-        halo_wait(e, 0)
-        halo_wait(e, 1)
-
-        def body(i, pairs):
-            rise = jnp.full(g_up.shape[1:], 1e-12, jnp.float32)
-            fall = rise
-            for minus, plus in pairs:
-                other = -plus
-                hi = jnp.maximum(jnp.maximum(minus, other), 0.0)
-                lo = jnp.minimum(jnp.minimum(minus, other), 0.0)
-                rise = rise + hi * hi
-                fall = fall + lo * lo
-            g_up[i] = jnp.sqrt(rise)
-            g_down[i] = jnp.sqrt(fall)
-
-        loop_slab(length, ext, e, body)
+                size = jnp.sqrt((base_size[i, at] + v * v) * ninth + 1e-12)
+                sign = start * lax.rsqrt(start * start + 1.0)
+                ext[e + 1, i + 3, at] = ext[e, i + 3, at] - redist_step * sign * (size - 1.0)
+
+        slab_pass(length, ext, e, body)
+        if not both:
+            halo_start(e + 1)
 
     def reply(it, p):
         src = out_b.at[it, p]
@@ -385,49 +412,64 @@
     def finish(it, body):
         pltpu.make_async_copy(resp.at[it], resp.at[it], r_recv.at[it]).wait()
 
-        def one(i, carry):
+        for i in range(length):
             s = u0[i] + gain[it, i] * resp[it, 0] + kbc[it, i] * resp[it, 1]
             cy, cz = cross[it, 0, i], cross[it, 1, i]
             near_y = jnp.where(cy > 0.0, shift(s, -1, 0), shift(s, 1, 0))
             near_z = jnp.where(cz > 0.0, shift(s, -1, 1), shift(s, 1, 1))
             body(i, s - (jnp.abs(cy) * (s - near_y) + jnp.abs(cz) * (s - near_z)))
-            return carry
-
-        lax.fori_loop(0, length, one, 0)
 
     def keep_speed(i, s):
         speed[i] = s
 
+    inner = range(1, length - 1)
+    for copy in loads[:3]:
+        copy.wait()
+    plane_rates(0, inner)
+    for copy in loads[3:]:
+        copy.wait()
+    raw_speed()
+    pl.semaphore_wait(barrier, met)
+    halo_start(0)
+    across(0)
     coefficients(0)
     sweeps(0)
-    for it in range(ITERS):
-        last = it == ITERS - 1
-        if not last:
-            redistance(it)
-            own(it)
-            if it == 0:
-                own_power()
-            coefficients(it + 1)
-            if it + 1 == ITERS - 1:
-                redistance(it + 1)
-            finish(it, keep_speed)
-            sweeps(it + 1)
-        else:
-            both_sizes(it + 1)
-            own(it)
+    send_power()
+    along(0)
+    plane_rates(1, inner)
+    across(1)
+    own(0)
+    own_power()
+    coefficients(1)
+    along(1)
+    across(2)
+    finish(0, keep_speed)
+    sweeps(1)
+    along(2)
+    own(1)
 
     pltpu.make_async_copy(pow_res, pow_res, q_recv.at[0]).wait()
     cells = length * decay.shape[0] * decay.shape[1] * n
     total = jnp.sum(pow_res[...], keepdims=True)
     scale = lax.rsqrt(total * (1.0 / cells) + 1e-06)
+
+    outs = [
+        (pltpu.make_async_copy(src.at[i], dst.at[i], out_sem.at[k, i]))
+        for i in range(length)
+        for k, (src, dst) in enumerate(((moved_out, moved_hbm), (speed_out, speed_hbm)))
+    ]
 
     def emit(i, s):
         s = s * scale
         speed_out[i] = s
         size = jnp.where(s >= 0.0, g_up[i], g_down[i])
         moved_out[i] = ext[ITERS, i + 3] - move_step * s * size
+        outs[2 * i].start()
+        outs[2 * i + 1].start()
 
     finish(ITERS - 1, emit)
+    for copy in outs:
+        copy.wait()
 
     for e in range(ITERS + 1):
         for part in range(2):
@@ -481,13 +523,13 @@
         vm = lambda *shape: pltpu.VMEM(shape, f32)
         sems = lambda *shape: pltpu.SemaphoreType.DMA(shape)
         any_ = pl.BlockSpec(memory_space=pl.ANY)
-        vmem = pl.BlockSpec(memory_space=pltpu.VMEM)
         return pl.pallas_call(
             functools.partial(kernel, n, base),
             out_shape=(jax.ShapeDtypeStruct(slab, f32), jax.ShapeDtypeStruct(slab, f32)),
-            in_specs=[any_] * 5 + [pl.BlockSpec(memory_space=pltpu.SMEM), vmem],
-            out_specs=(vmem, vmem),
+            in_specs=[any_] * 7,
+            out_specs=(any_, any_),
             scratch_shapes=[
+                pltpu.SMEM(contrast.shape, f32), vm(depth, height), vm(*slab), vm(*slab), vm(*slab),
                 vm(*forward.shape), vm(*adjoint.shape),
                 pltpu.VMEM(slab, jnp.int32), pltpu.VMEM(signs.shape, jnp.int32),
                 vm(ITERS + 1, length + 6, depth, height),
@@ -498,9 +540,10 @@
                 vm(ITERS, n, 3, rows, height), vm(ITERS, n, 2, rows, height),
                 vm(ITERS, n, 2, rows, height), vm(ITERS, 2, depth, height),
                 vm(8, height), vm(n, 8, height), vm(8, height), vm(8, height),
-                sems(5), sems(ITERS + 1, 2, 2), sems(ITERS + 1, 2, 2),
+                sems(7), sems(ITERS + 1, 2, 2), sems(ITERS + 1, 2, 2),
                 sems(ITERS, OWNERS), sems(ITERS), sems(ITERS, OWNERS), sems(ITERS),
                 sems(ITERS, n), sems(ITERS), sems(1), sems(1), sems(n), sems(1),
+                sems(2, length),
             ],
             compiler_params=pltpu.CompilerParams(collective_id=0, has_side_effects=True),
         )(forward, adjoint, level, labels, signs, contrast, decay)

time: 35.7 us -> 28.7 us (0.80)
  Pallas kernels: 32.6 us -> 25.6 us
    pallas_call x1, Pallas kernels: 32.6 us -> 25.6 us  [shards(): pl.pallas_call(functools.partial(kernel, n, base), out_shape=(jax.ShapeDt...]
where the time goes in v2:
time: 28.7 us; the launch traced here: 28.5 us
  Pallas kernels  25.6 us (89%)
  local copies, waits for them, and re-layouts  2.26 us (8%)
  between operations  0.65 us (2%)
    pallas_call x1, Pallas kernels, shards(): pl.pallas_call(functools.partial(kernel, n, base), out_shape=(jax.ShapeDt...  25.6 us
    unnamed x4, local copies, waits for them, and re-layouts  2.26 us

profile of v2, /device:TPU:0, one launch (start us, length us, event | category | flops | bytes accessed | tf_op | source)
XLA Modules:
  0.0 28.5 jit_solution(11012333006033315535)
XLA Ops:
  0.6 25.6 %shard_map.86 = (f32[8,32,128]{2,1,0:T(8,128)}, f32[8,32,128]{2,1,0:T(8,128)}) custom-call(f32[6,8,32,128]{3,2,1,0:T(8,128)} %fwd_hbm.1, f32[6,8,32,128]{3,2,1,0:T(8,128)} %adj_hbm.1, f32[8,32,128]{2,1,0:T(8,128)} %lvl_hbm.1, s32[8,32,128]{2,1,0:T(8,128)} %lab_hbm.1, s32[3,8,32,128]{3,2,1,0:T(8,128)} %sgn_hbm.1, f32[4]{0:T(128)} %contrast_hbm.1, ...), custom_call_target="tpu_custom_call" | custom-call | tf_op jit(solution)/shard_map/pallas_call | solution.py:526
  26.3 0.0 copy-start
  26.3 1.6 %copy.11 = f32[8,32,128]{2,1,0:T(8,128)} copy(f32[8,32,128]{2,1,0:T(8,128)} %get-tuple-element.4) | data formatting | bytes 262144
  27.9 0.0 copy-done
  27.9 0.7 %copy.12 = f32[8,32,128]{2,1,0:T(8,128)} copy(f32[8,32,128]{2,1,0:T(8,128)S(1)} %copy-done) | data formatting | bytes 262144
Async XLA Ops:
  26.3 1.6 %copy-start = (f32[8,32,128]{2,1,0:T(8,128)S(1)}, f32[8,32,128]{2,1,0:T(8,128)}, u32[]{:S(2)}) copy-start(f32[8,32,128]{2,1,0:T(8,128)} %get-tuple-element.5) | copy-start | bytes 393220

commit v3 on v2

--- a/solution.py
+++ b/solution.py
@@ -81,12 +81,12 @@
 def kernel(
     n, base,
     fwd_hbm, adj_hbm, lvl_hbm, lab_hbm, sgn_hbm, contrast_hbm, decay_hbm,
-    moved_hbm, speed_hbm,
-    contrast, decay, moved_out, speed_out, base_size,
+    moved_out, speed_out,
+    contrast, decay, base_size,
     fwd, adj, lab, sgn, ext, speed, kf, pf, kb, pb, kfc, cross, gain, kbc, u0, g_up, g_down,
     snd_c, snd_s, in_c, in_s, out_b, resp, pow_s, pow_in, pow_out, pow_res,
     load_sem, halo_send, halo_recv, c_send, c_recv, s_send, s_recv, r_send, r_recv,
-    p_send, p_recv, q_send, q_recv, out_sem,
+    p_send, p_recv, q_send, q_recv,
 ):
     me = lax.axis_index("gx")
     corner = lax.axis_index("corner")
@@ -453,24 +453,13 @@
     total = jnp.sum(pow_res[...], keepdims=True)
     scale = lax.rsqrt(total * (1.0 / cells) + 1e-06)
 
-    outs = [
-        (pltpu.make_async_copy(src.at[i], dst.at[i], out_sem.at[k, i]))
-        for i in range(length)
-        for k, (src, dst) in enumerate(((moved_out, moved_hbm), (speed_out, speed_hbm)))
-    ]
-
     def emit(i, s):
         s = s * scale
         speed_out[i] = s
         size = jnp.where(s >= 0.0, g_up[i], g_down[i])
         moved_out[i] = ext[ITERS, i + 3] - move_step * s * size
-        outs[2 * i].start()
-        outs[2 * i + 1].start()
 
     finish(ITERS - 1, emit)
-    for copy in outs:
-        copy.wait()
-
     for e in range(ITERS + 1):
         for part in range(2):
             for side in range(2):
@@ -513,7 +502,7 @@
 
 def solution(mesh):
     n = mesh.shape["gx"]
-    base = n // 2 - OWNERS
+    base = n // 2 - OWNERS + 1
 
     def shards(forward, adjoint, level, labels, signs, contrast, decay):
         slab = level.shape
@@ -525,11 +514,11 @@
         any_ = pl.BlockSpec(memory_space=pl.ANY)
         return pl.pallas_call(
             functools.partial(kernel, n, base),
-            out_shape=(jax.ShapeDtypeStruct(slab, f32), jax.ShapeDtypeStruct(slab, f32)),
+            out_shape=(pltpu.VMEM(slab, f32), pltpu.VMEM(slab, f32)),
             in_specs=[any_] * 7,
-            out_specs=(any_, any_),
+            out_specs=(pl.BlockSpec(memory_space=pltpu.VMEM),) * 2,
             scratch_shapes=[
-                pltpu.SMEM(contrast.shape, f32), vm(depth, height), vm(*slab), vm(*slab), vm(*slab),
+                pltpu.SMEM(contrast.shape, f32), vm(depth, height), vm(*slab),
                 vm(*forward.shape), vm(*adjoint.shape),
                 pltpu.VMEM(slab, jnp.int32), pltpu.VMEM(signs.shape, jnp.int32),
                 vm(ITERS + 1, length + 6, depth, height),
@@ -543,7 +532,6 @@
                 sems(7), sems(ITERS + 1, 2, 2), sems(ITERS + 1, 2, 2),
                 sems(ITERS, OWNERS), sems(ITERS), sems(ITERS, OWNERS), sems(ITERS),
                 sems(ITERS, n), sems(ITERS), sems(1), sems(1), sems(n), sems(1),
-                sems(2, length),
             ],
             compiler_params=pltpu.CompilerParams(collective_id=0, has_side_effects=True),
         )(forward, adjoint, level, labels, signs, contrast, decay)

time: 28.7 us -> 25.4 us (0.89)
  Pallas kernels: 25.6 us -> 23.3 us
  local copies, waits for them, and re-layouts: 2.26 us -> 1.31 us
    pallas_call x1, Pallas kernels: 25.6 us -> 23.3 us  [shards(): pl.pallas_call(functools.partial(kernel, n, base), out_shape=(pltpu.VMEM(...]
    unnamed x4 -> x2, local copies, waits for them, and re-layouts: 2.26 us -> 1.31 us
where the time goes in v3:
time: 25.4 us; the launch traced here: 25.3 us
  Pallas kernels  23.3 us (92%)
  local copies, waits for them, and re-layouts  1.31 us (5%)
  between operations  0.64 us (3%)
    pallas_call x1, Pallas kernels, shards(): pl.pallas_call(functools.partial(kernel, n, base), out_shape=(pltpu.VMEM(...  23.3 us
    unnamed x2, local copies, waits for them, and re-layouts  1.31 us

profile of v3, /device:TPU:0, one launch (start us, length us, event | category | flops | bytes accessed | tf_op | source)
XLA Modules:
  0.0 25.3 jit_solution(9454412917880504829)
XLA Ops:
  0.6 23.3 %shard_map.86 = (f32[8,32,128]{2,1,0:T(8,128)S(1)}, f32[8,32,128]{2,1,0:T(8,128)S(1)}) custom-call(f32[6,8,32,128]{3,2,1,0:T(8,128)} %fwd_hbm.1, f32[6,8,32,128]{3,2,1,0:T(8,128)} %adj_hbm.1, f32[8,32,128]{2,1,0:T(8,128)} %lvl_hbm.1, s32[8,32,128]{2,1,0:T(8,128)} %lab_hbm.1, s32[3,8,32,128]{3,2,1,0:T(8,128)} %sgn_hbm.1, f32[4]{0:T(128)} %contrast_hbm.1, ...), custom_call_target="tpu_custom_call" | custom-call | tf_op jit(solution)/shard_map/pallas_call | solution.py:515
  23.9 0.7 %copy.11 = f32[8,32,128]{2,1,0:T(8,128)} copy(f32[8,32,128]{2,1,0:T(8,128)S(1)} %get-tuple-element.2) | data formatting | bytes 262144
  24.6 0.7 %copy.12 = f32[8,32,128]{2,1,0:T(8,128)} copy(f32[8,32,128]{2,1,0:T(8,128)S(1)} %get-tuple-element.3) | data formatting | bytes 262144

commit v4 on v3

--- a/solution.py
+++ b/solution.py
@@ -426,11 +426,11 @@
     for copy in loads[:3]:
         copy.wait()
     plane_rates(0, inner)
+    pl.semaphore_wait(barrier, met)
+    halo_start(0)
     for copy in loads[3:]:
         copy.wait()
     raw_speed()
-    pl.semaphore_wait(barrier, met)
-    halo_start(0)
     across(0)
     coefficients(0)
     sweeps(0)

time: 25.4 us -> 25.4 us (level)
  no operation moved by 1% of the time
where the time goes in v4:
time: 25.4 us; the launch traced here: 25.3 us
  Pallas kernels  23.3 us (92%)
  local copies, waits for them, and re-layouts  1.31 us (5%)
  between operations  0.64 us (3%)
    pallas_call x1, Pallas kernels, shards(): pl.pallas_call(functools.partial(kernel, n, base), out_shape=(pltpu.VMEM(...  23.3 us
    unnamed x2, local copies, waits for them, and re-layouts  1.31 us

profile of v4, /device:TPU:0, one launch (start us, length us, event | category | flops | bytes accessed | tf_op | source)
XLA Modules:
  0.0 25.3 jit_solution(871612787773274321)
XLA Ops:
  0.6 23.3 %shard_map.86 = (f32[8,32,128]{2,1,0:T(8,128)S(1)}, f32[8,32,128]{2,1,0:T(8,128)S(1)}) custom-call(f32[6,8,32,128]{3,2,1,0:T(8,128)} %fwd_hbm.1, f32[6,8,32,128]{3,2,1,0:T(8,128)} %adj_hbm.1, f32[8,32,128]{2,1,0:T(8,128)} %lvl_hbm.1, s32[8,32,128]{2,1,0:T(8,128)} %lab_hbm.1, s32[3,8,32,128]{3,2,1,0:T(8,128)} %sgn_hbm.1, f32[4]{0:T(128)} %contrast_hbm.1, ...), custom_call_target="tpu_custom_call" | custom-call | tf_op jit(solution)/shard_map/pallas_call | solution.py:515
  24.0 0.7 %copy.11 = f32[8,32,128]{2,1,0:T(8,128)} copy(f32[8,32,128]{2,1,0:T(8,128)S(1)} %get-tuple-element.2) | data formatting | bytes 262144
  24.6 0.7 %copy.12 = f32[8,32,128]{2,1,0:T(8,128)} copy(f32[8,32,128]{2,1,0:T(8,128)S(1)} %get-tuple-element.3) | data formatting | bytes 262144
